TPU v7x, 32 devices: a whole 2x2x4 slice. The times are simulated.
32 devices in a mesh: lon: 4 (over y, x), lat: 8 (over z, core).
Axes of the slice: x: 2, y: 2, z: 4, core: 2. Of those that a mesh axis runs over, the one named last changes fastest.
Arguments:
- spectrum: float32 [32, 512, 648], P('lon', 'lat'), may hold values from 0.01 to 1
- sea_mask: int32 [32, 512], P('lon', 'lat'), may hold values from 0 to 1, as said below
- ice_flags: int32 [32, 512], P('lon', 'lat'), may hold values 0 or 1
- wind_forcing: float32 [32, 512], P('lon', 'lat'), may hold values from 0.1 to 1.5
- group_speed: float32 [18], replicated, may hold values from 0.3 to 1
- coupling: bfloat16 [648, 648], replicated, may hold values from -0.25 to 0.25
Outputs:
- field: float32 [32, 512, 648], P('lon', 'lat')
Inputs may be any that keep to these rules, and one draw needn't show every extreme that they name: `sea_mask`: each device's block of 8 x 64 cells holds at most 384 sea cells and at least 128; in every draw some block holds exactly 384.
All inputs are finite; a program needn't handle non-finite values. No bound on the sum of `ice_flags` on one device may be relied on, other than what follows from the above.
Results may differ from a plain program's by a relative error of at most 0.00079.
Values sent between devices are 32-bit elements; how exact they have to be, the bound alone decides.
No kernel may reach another device: no remote copies, remote signals or barrier semaphores. Data moves between devices by JAX's collectives and lax.ppermute only.
A program may use at most 64 MiB of HBM per device.

v0:
```python
import functools
import math

import jax
import jax.numpy as jnp
import numpy as np
from jax import lax
from jax.experimental import pallas as pl
from jax.experimental.pallas import tpu as pltpu
from jax.sharding import PartitionSpec as P


DIRS = 36
STEPS = 4
LANES = 128
DEPTH = 4

time_step = 0.2
dissipation = 0.5

VMEM = pltpu.VMEM
SMEM = pltpu.SMEM


def swap_pairs(size, first, wrap):
    pairs = []
    for i in range(first, size, 2):
        j = i + 1
        if j >= size:
            if not wrap:
                continue
            j = j % size
        pairs += [(i, j), (j, i)]
    return pairs


def lane_tiles(bins):
    return pl.cdiv(bins, LANES)


def lanes_of(tile):
    return slice(tile * LANES, (tile + 1) * LANES)


def lane_index(shape):
    return lax.broadcasted_iota(jnp.int32, shape, 1)


def row_index(shape):
    return lax.broadcasted_iota(jnp.int32, shape, 0)


def eastward(bins, tile, shape):
    bin_here = lane_index(shape) + tile * LANES
    quarter = bins // 4
    return (bin_here < quarter) | (bin_here >= bins - quarter)


def northward(bins, tile, shape):
    return lane_index(shape) + tile * LANES < bins // 2


def kinds(bins, tile, test):
    low, high = tile * LANES, min((tile + 1) * LANES, bins)
    return {bool(test(b)) for b in range(low, high)}


def is_east(bins):
    return lambda b: b < bins // 4 or b >= bins - bins // 4


def is_north(bins):
    return lambda b: b < bins // 2


def upwind_lat(f, bins, tile):
    shape = f.shape
    rows = shape[0]
    found = kinds(bins, tile, is_north(bins))
    south = pltpu.roll(f, 1, 0) if True in found else None
    north = pltpu.roll(f, rows - 1, 0) if False in found else None
    if south is None:
        return north
    if north is None:
        return south
    return jnp.where(northward(bins, tile, shape), south, north)


def advect(f, across, stay, go_x, go_y, bins, tile):
    along = upwind_lat(f, bins, tile)
    return stay * f + go_x * across + go_y * along


def turn(value, shift):
    shift = shift % LANES
    return pltpu.roll(value, shift, 1) if shift else value


def pack_plan(bins, west):
    split = bins // 4 - LANES
    high = bins - bins // 4 - 3 * LANES
    width = 2 * split
    return split, high, width, LANES - width, (split if west else high)


def pack_count(rows, halo):
    blocks = rows // 8
    return 2 * blocks + blocks // 2 + 1 + (2 if halo else 0)


def half_parts(t, west, bins):
    split, high, _, _, _ = pack_plan(bins, west)
    lane = lane_index(t[0].shape)
    if west:
        return t[2], jnp.where(lane < high, t[3], t[1]), t[1]
    return t[0], t[4], jnp.where(lane < split, t[1], jnp.where(lane >= high, t[3], turn(t[5], split)))


def pack_half(tiles, west, bins, rows, halo, out):
    _, _, width, kept, start = pack_plan(bins, west)
    rest = width - kept
    blocks = rows // 8
    half = blocks // 2
    lane = lane_index((8, LANES))

    left = jnp.zeros((8, LANES), jnp.float32)
    held = {}
    for block in range(blocks + (1 if halo else 0)):
        full, other, part = half_parts([tile[8 * block : 8 * block + 8] for tile in tiles], west, bins)
        if block < blocks:
            out[block] = full
            out[blocks + block] = other
            if block < half:
                held[block] = turn(part, -start)
            else:
                k = block - half
                out[2 * blocks + k] = jnp.where(lane < width, held.pop(k), turn(part, width - start))
                low = rest * k
                left = jnp.where((lane >= low) & (lane < low + rest), turn(part, low - kept - start), left)
        else:
            left = jnp.where(lane >= half * rest, turn(part, half * rest - start), left)
            out[2 * blocks + half + 1] = full
            out[2 * blocks + half + 2] = other
    out[2 * blocks + half] = left


def pack_corner(parts, before, west, bins, rows, out):
    _, _, width, kept, start = pack_plan(bins, west)
    rest = width - kept
    half = rows // 16
    spot = 5 * half
    lane = lane_index((8, LANES))
    out[spot] = jnp.where(lane >= half * rest, turn(parts[2], half * rest - start), before[spot])
    out[spot + 1] = parts[0]
    out[spot + 2] = parts[1]


def across_edge(halo, inner, west, bins, rows, with_halo, corner=None):
    split, high, width, kept, start = pack_plan(bins, not west)
    rest = width - kept
    blocks = rows // 8
    half = blocks // 2
    lane = lane_index((8, LANES))
    left = halo[2 * blocks + half]
    found = [[] for _ in inner]
    for block in range(blocks + 1):
        near = [tile[8 * block : 8 * block + 8] for tile in inner]
        if block == blocks and not with_halo:
            new = near
        else:
            if block == blocks and corner is not None:
                full, other, part = corner[0], corner[1], corner[2]
            elif block == blocks:
                full, other = halo[2 * blocks + half + 1], halo[2 * blocks + half + 2]
                part = turn(left, start - half * rest)
            else:
                full, other = halo[block], halo[blocks + block]
                if block < half:
                    part = turn(halo[2 * blocks + block], start)
                else:
                    k = block - half
                    early = (lane >= high) | (lane < split) if west else lane < start + kept
                    part = jnp.where(early, turn(halo[2 * blocks + k], start - width), turn(left, start + kept - rest * k))
            if west:
                new = [
                    full, jnp.where(lane < split, part, near[1]), near[2],
                    jnp.where(lane >= high, part, near[3]), other, turn(part, -split),
                ]
            else:
                new = [
                    near[0], jnp.where(lane < split, near[1], jnp.where(lane < high, part, other)), full,
                    jnp.where(lane < high, other, near[3]), near[4], near[5],
                ]
        for k, value in enumerate(new):
            found[k].append(value)
    return [jnp.concatenate(values, axis=0) for values in found]


def on_each_side(second, body):
    west = west_flag(second)

    @pl.when(west)
    def _():
        body(True)

    @pl.when(jnp.logical_not(west))
    def _():
        body(False)


def west_flag(second):
    odd = lax.rem(lax.axis_index("lon"), 2)
    return (1 - odd if second else odd) == 1


def south_flag(second):
    odd = lax.rem(lax.axis_index("lat"), 2)
    return (1 - odd if second else odd) == 1


def read_tile(ref, where, bins, tile):
    low, high = tile * LANES, min((tile + 1) * LANES, bins)
    value = ref[where + (slice(None), slice(low, high))]
    if high - low == LANES:
        return value
    return jnp.concatenate([value, jnp.zeros((value.shape[0], LANES - (high - low)), value.dtype)], axis=1)


def write_tile(ref, where, bins, tile, value):
    rows, low, high = ref.shape[-2], tile * LANES, min((tile + 1) * LANES, bins)
    ref[where + (slice(None), slice(low, high))] = value[:rows, : high - low]


def masks_kernel_part(sea_ref, ice_ref, wind_ref):
    sea = sea_ref[...].astype(jnp.float32)
    gain = 1.0 + time_step * (wind_ref[...] * (1.0 - ice_ref[...].astype(jnp.float32)))
    _, rows = sea.shape
    sea = jnp.concatenate([sea, gain], axis=1)
    turned = jnp.transpose(sea)
    return turned[:rows], turned[rows:]


def first_kernel(bins, spectrum, sea_hbm, ice_hbm, wind_hbm, out_a, out_b, edge, sea_ref, ice_ref, wind_ref, sems):
    columns, rows = sea_ref.shape
    copies = []
    masks = [
        pltpu.make_async_copy(source, target, sems.at[2 + k])
        for k, (source, target) in enumerate(((sea_hbm, sea_ref), (ice_hbm, ice_ref), (wind_hbm, wind_ref)))
    ]
    for copy in masks:
        copy.start()
    for c in range(columns):
        for k, start in enumerate((0, rows - 8)):
            copy = pltpu.make_async_copy(spectrum.at[c, pl.ds(start, 8)], edge.at[k, c], sems.at[k])
            copy.start()
            copies.append(copy)
    for copy in masks:
        copy.wait()
    sea, gain = masks_kernel_part(sea_ref, ice_ref, wind_ref)
    shape = (8, LANES)
    lane = lane_index(shape)
    row = row_index(shape)
    used = bins % LANES
    for copy in copies:
        copy.wait()
    tiles = lane_tiles(bins)
    space = LANES // (columns // 2)
    for second, out in ((False, out_a), (True, out_b)):
        to_south = south_flag(second)
        ends = jnp.zeros(shape, jnp.float32)
        for pair in range(columns // 2):
            for tile in range(tiles):
                halves = []
                for c in (2 * pair, 2 * pair + 1):
                    low, high = read_tile(edge, (0, c), bins, tile), read_tile(edge, (1, c), bins, tile)
                    here = jnp.where(to_south, low, high)
                    s = jnp.where(to_south, sea[0:8, c : c + 1], sea[rows - 8 : rows, c : c + 1])
                    s = jnp.broadcast_to(s, shape)
                    value = here * s
                    if tile == tiles - 1:
                        g = jnp.where(to_south, gain[0:8, c : c + 1], gain[rows - 8 : rows, c : c + 1])
                        g = jnp.broadcast_to(g, shape)
                        value = jnp.where(lane < used, value, jnp.where(lane == used, s, g))
                    halves.append(value)
                first, other = halves
                keep = (row < DEPTH) == to_south
                value = jnp.where(keep, first, pltpu.roll(other, DEPTH, 0))
                if tile < tiles - 1:
                    out[pair * (tiles - 1) + tile] = value
                else:
                    here = (lane >= pair * space) & (lane < (pair + 1) * space)
                    ends = jnp.where(here, turn(value, pair * space), ends)
        out[columns // 2 * (tiles - 1)] = ends


def table_kernel(bins, rows, speed_ref, angle_ref, coupling_ref, stay, go_x, go_y, wide):
    tiles = lane_tiles(bins)
    padded = tiles * LANES
    used = bins % LANES
    shape = (rows + 2 * DEPTH, LANES)
    row = row_index(shape)
    here = jnp.where(row >= rows + DEPTH, row - rows - 2 * DEPTH, row) + lax.axis_index("lat") * rows
    total = rows * lax.axis_size("lat")
    latitude = (-60.0 + 120.0 * (here.astype(jnp.float32) + 0.5) / total) * (math.pi / 180.0)
    over = 1.0 / jnp.cos(latitude)
    count = speed_ref.shape[0]
    for tile in range(tiles):
        which = angle_ref[2:3, lanes_of(tile)]
        speed = jnp.zeros((1, LANES), jnp.float32)
        for k in range(count):
            speed = jnp.where(which == float(k), speed_ref[k], speed)
        x = (angle_ref[0:1, lanes_of(tile)] * speed) * over
        y = angle_ref[1:2, lanes_of(tile)] * speed
        go_x[:, lanes_of(tile)] = x
        go_y[:, lanes_of(tile)] = jnp.broadcast_to(y, (8, LANES))
        stay[:, lanes_of(tile)] = 1.0 - x - y
    body = bins - used
    wide[:, :body] = jnp.concatenate(
        [coupling_ref[:, :body], jnp.zeros((padded - bins, body), jnp.bfloat16)], axis=0
    )
    tail = jnp.concatenate([coupling_ref[:, body:], jnp.ones((bins, padded - bins), jnp.bfloat16)], axis=1)
    wide[:, body:] = jnp.concatenate([tail, jnp.zeros((padded - bins, LANES), jnp.bfloat16)], axis=0)


def load_kernel(bins, spectrum, sea_ref, ice_ref, wind_ref, edge_a, edge_b, inner, seas, gains, pack_a, pack_b):
    columns, rows = sea_ref.shape
    tiles = lane_tiles(bins)
    used = bins % LANES
    sea, gain = masks_kernel_part(sea_ref, ice_ref, wind_ref)
    for c in range(columns):
        s = jnp.broadcast_to(sea[:, c : c + 1], (rows, LANES))
        seas[c, :rows] = time_step * s
        gains[c, :rows] = s * jnp.broadcast_to(gain[:, c : c + 1], (rows, LANES))
    lane = lane_index((rows, LANES))

    def put(target, c):
        s = seas[c, :rows] != 0.0
        for tile in range(tiles):
            value = read_tile(spectrum, (c,), bins, tile)
            keep = s
            if tile == tiles - 1:
                keep = s & (lane < used)
            target[:rows, lanes_of(tile)] = jnp.where(keep, value, 0.0)

    for c in range(1, columns - 1):
        put(inner.at[c - 1], c)
    for second, target, pack in ((False, edge_a, pack_a), (True, edge_b, pack_b)):

        def side(west, target=target, pack=pack):
            put(target, 0 if west else columns - 1)
            pack_half([target[:rows, lanes_of(t)] for t in range(tiles)], west, bins, rows, False, pack)

        on_each_side(second, side)


def halo_rows(bins, from_a, from_b, slot, seas, gains, column):
    tiles = lane_tiles(bins)
    rows = seas.shape[1] - 2 * DEPTH
    used = bins % LANES
    shape = (8, LANES)
    top = row_index(shape) < DEPTH
    a_south = south_flag(False)
    values = []
    for tile in range(tiles):
        here = []
        for ref, pairs, index in (from_a, from_b):
            if tile < tiles - 1:
                here.append(ref[index * (tiles - 1) + tile])
            else:
                here.append(turn(ref[pairs * (tiles - 1)], -index * (LANES // pairs)))
        low, high = jnp.where(a_south, here[0], here[1]), jnp.where(a_south, here[1], here[0])
        if slot:
            low, high = pltpu.roll(low, DEPTH, 0), pltpu.roll(high, DEPTH, 0)
        values.append(jnp.where(top, high, low))
    last = values[-1]
    s = jnp.broadcast_to(last[:, used : used + 1], shape)
    g = jnp.broadcast_to(last[:, used + 1 : used + 2], shape)
    seas[column, rows:] = time_step * s
    gains[column, rows:] = s * g
    values[-1] = jnp.where(lane_index(shape) < used, last, 0.0)
    return values


def corner_kernel(bins, after, halo_a, halo_b, edge_in, seas_in, gains_in, edge, seas, gains, corner):
    columns = seas.shape[0]
    rows = seas.shape[1] - 2 * DEPTH

    def side(west):
        c = 0 if west else columns - 1
        at = (columns // 2, c // 2)
        mine = halo_rows(bins, (halo_a,) + at, (halo_b,) + at, c % 2, seas, gains, c)
        for tile, value in enumerate(mine):
            edge[rows:, lanes_of(tile)] = value
        for k, value in enumerate(half_parts(mine, west, bins)):
            corner[k] = value

    on_each_side(True, side)


def join_kernel(
    bins, halo_a, halo_b, edge_in, inner_in, seas_in, gains_in, pack_in, edge, inner, seas, gains, pack
):
    columns = seas.shape[0]
    rows = seas.shape[1] - 2 * DEPTH

    def column(c):
        at = (columns // 2, c // 2)
        return halo_rows(bins, (halo_a,) + at, (halo_b,) + at, c % 2, seas, gains, c)

    def side(west):
        mine = column(0 if west else columns - 1)
        for tile, value in enumerate(mine):
            edge[rows:, lanes_of(tile)] = value
        pack_corner(half_parts(mine, west, bins), pack_in, west, bins, rows, pack)

    on_each_side(False, side)
    for c in range(1, columns - 1):
        for tile, value in enumerate(column(c)):
            inner[c - 1, rows:, lanes_of(tile)] = value


def ordered_first_kernel(bins, second, after, corner, *refs):
    edge_kernel(bins, second, *refs, corner=corner)


def ordered_edge_kernel(bins, second, after, *refs):
    edge_kernel(bins, second, *refs)


def edge_kernel(
    bins, second, halo, edge, inner, seas, gains, stay, go_x, go_y, wide, out, pack, adv_ref, corner=None
):
    rows = edge.shape[0] - 2 * DEPTH
    halo_next = pack.shape[0] == pack_count(rows, True)

    def side(west):
        fresh = edge_step(bins, west, halo, edge, inner, seas, gains, stay, go_x, go_y, wide, adv_ref, False, corner)
        for t, value in enumerate(fresh):
            out[:, lanes_of(t)] = value
        pack_half(fresh, west, bins, rows, halo_next, pack)

    on_each_side(second, side)


def ordered_late_kernel(bins, second, after, *refs):
    late_edge_kernel(bins, second, *refs)


def late_edge_kernel(bins, second, halo, edge, inner, seas, gains, stay, go_x, go_y, wide, out, adv_ref):
    def side(west):
        fresh = edge_step(bins, west, halo, edge, inner, seas, gains, stay, go_x, go_y, wide, adv_ref, True)
        for t, value in enumerate(fresh):
            write_tile(out, (), bins, t, value)

    on_each_side(second, side)


def last_edge_kernel(
    bins, second, halo, edge, inner, seas, gains, stay, go_x, go_y, wide, done_inner, done_edge, out, adv_ref, column, sems
):
    columns = out.shape[0]
    mine = jnp.where(west_flag(second), 0, columns - 1)
    copies = [
        pltpu.make_async_copy(done_inner, out.at[pl.ds(1, columns - 2)], sems.at[0]),
        pltpu.make_async_copy(done_edge, out.at[columns - 1 - mine], sems.at[1]),
    ]
    for copy in copies:
        copy.start()
    late_edge_kernel(bins, second, halo, edge, inner, seas, gains, stay, go_x, go_y, wide, column, adv_ref)
    copies.append(pltpu.make_async_copy(column, out.at[mine], sems.at[2]))
    copies[2].start()
    for copy in copies:
        copy.wait()


def edge_step(bins, west, halo, edge, inner, seas, gains, stay, go_x, go_y, wide, adv_ref, last, corner=None):
    tiles = lane_tiles(bins)
    columns = inner.shape[0] + 2
    rows = edge.shape[0] - 2 * DEPTH
    used = rows if last else edge.shape[0]
    near, mine = (0, 0) if west else (columns - 3, columns - 1)
    across = across_edge(halo, [inner[near, :, lanes_of(t)] for t in range(tiles)], west, bins, rows, not last, corner)
    for t in range(tiles):
        here = lanes_of(t)
        adv = advect(edge[:, here], across[t], stay[:, here], go_x[:, here], go_y[0:1, here], bins, t)
        adv_ref[:used, here] = adv[:used]
    low = adv_ref[:used].astype(jnp.bfloat16)
    s, g = seas[mine, :used], gains[mine, :used]
    fresh = [None] * tiles
    keep = None
    for block in lane_blocks(tiles):
        product = jnp.dot(low, wide[:, block[0] * LANES : (block[-1] + 1) * LANES], preferred_element_type=jnp.float32)
        if keep is None:
            share = jnp.broadcast_to(product[:, -1:], (used, LANES)) * (dissipation / bins)
            keep = g - s * share
        for k, t in enumerate(block):
            fresh[t] = adv_ref[:used, lanes_of(t)] * keep + s * product[:, lanes_of(k)]
    return fresh


def lane_blocks(tiles):
    return [(t - 1, t) for t in range(tiles - 1, 0, -2)]


def inner_kernel(bins, edge_a, edge_b, inner, seas, gains, stay, go_x, go_y, wide, out, adv_ref, low_ref, keep_ref):
    tiles = lane_tiles(bins)
    count, tall = inner.shape[0], inner.shape[1]
    rows = adv_ref.shape[0] // count
    a_west = west_flag(False)
    parts = 2
    if count % parts:
        parts = 1
    for part in range(parts):
        group = range(part * count // parts, (part + 1) * count // parts)
        whole = slice(group[0] * rows, (group[-1] + 1) * rows)
        for t in range(tiles):
            here = lanes_of(t)
            found = kinds(bins, t, is_east(bins))
            for c in group:
                west = east = None
                if True in found:
                    west = inner[c - 1, :, here] if c else jnp.where(a_west, edge_a[:, here], edge_b[:, here])
                if False in found:
                    east = inner[c + 1, :, here] if c < count - 1 else jnp.where(a_west, edge_b[:, here], edge_a[:, here])
                if west is None:
                    across = east
                elif east is None:
                    across = west
                else:
                    across = jnp.where(eastward(bins, t, (tall, LANES)), west, east)
                adv = advect(inner[c, :, here], across, stay[:, here], go_x[:, here], go_y[0:1, here], bins, t)[:rows]
                adv_ref[c * rows : (c + 1) * rows, here] = adv
        low_ref[whole] = adv_ref[whole].astype(jnp.bfloat16)
        for block in lane_blocks(tiles):
            product = jnp.dot(
                low_ref[whole], wide[:, block[0] * LANES : (block[-1] + 1) * LANES], preferred_element_type=jnp.float32
            )
            for c in group:
                span = slice(c * rows, (c + 1) * rows)
                mine = slice((c - group[0]) * rows, (c - group[0] + 1) * rows)
                s = seas[c + 1, :rows]
                if block[-1] == tiles - 1:
                    share = jnp.broadcast_to(product[mine, -1:], (rows, LANES)) * (dissipation / bins)
                    keep_ref[span] = gains[c + 1, :rows] - s * share
                for k, t in enumerate(block):
                    value = adv_ref[span, lanes_of(t)] * keep_ref[span] + s * product[mine, lanes_of(k)]
                    if rows == tall:
                        out[c, :, lanes_of(t)] = value
                    else:
                        write_tile(out, (c,), bins, t, value)


def angle_table(bins, freqs):
    padded = lane_tiles(bins) * LANES
    table = np.zeros((8, padded), np.float32)
    theta = (np.arange(DIRS) + 0.5) * (2.0 * math.pi / DIRS)
    table[0, :bins] = np.repeat(0.225 * np.abs(np.cos(theta)), freqs)
    table[1, :bins] = np.repeat(0.45 * np.abs(np.sin(theta)), freqs)
    table[2, :] = -1.0
    table[2, :bins] = np.tile(np.arange(freqs), DIRS)
    return table


def steps(spectrum, sea_mask, ice_flags, wind_forcing, group_speed, coupling):
    columns, rows, bins = spectrum.shape
    tiles = lane_tiles(bins)
    padded = tiles * LANES
    tall = rows + 2 * DEPTH
    f32 = jnp.float32
    lon, lat = lax.axis_size("lon"), lax.axis_size("lat")
    lon_a, lon_b = swap_pairs(lon, 0, True), swap_pairs(lon, 1, True)
    lat_a, lat_b = swap_pairs(lat, 0, False), swap_pairs(lat, 1, False)
    vmem = pl.BlockSpec(memory_space=VMEM)
    smem = pl.BlockSpec(memory_space=SMEM)
    hbm = pl.BlockSpec(memory_space=pltpu.HBM)
    edge_shape = VMEM((tall, padded), f32)
    inner_shape = VMEM((columns - 2, tall, padded), f32)
    mask_shape = VMEM((columns, tall, LANES), f32)
    table_shape = VMEM((tall, padded), f32)

    def call(body, outs, ins, specs, scratch=(), aliases=None, flops=0, out_specs=None):
        return pl.pallas_call(
            body,
            out_shape=outs,
            in_specs=specs,
            out_specs=out_specs if out_specs is not None else jax.tree.map(lambda _: vmem, outs),
            scratch_shapes=list(scratch),
            input_output_aliases=aliases or {},
            cost_estimate=pl.CostEstimate(flops=flops, bytes_accessed=0, transcendentals=0),
            compiler_params=pltpu.CompilerParams(vmem_limit_bytes=24 * 1024 * 1024),
        )(*ins)

    send_a, send_b = call(
        functools.partial(first_kernel, bins),
        (VMEM((columns // 2 * (tiles - 1) + 1, 8, LANES), f32),) * 2,
        [pltpu.with_memory_space_constraint(x, pltpu.HBM) for x in (spectrum, sea_mask, ice_flags, wind_forcing)],
        [hbm] * 4,
        [VMEM((2, columns, 8, bins), f32), VMEM((columns, rows), sea_mask.dtype), VMEM((columns, rows), ice_flags.dtype),
         VMEM((columns, rows), f32), pltpu.SemaphoreType.DMA((5,))],
    )
    halo_b = lax.ppermute(send_b, "lat", lat_b)
    halo_a = lax.ppermute(send_a, "lat", lat_a)
    pack_own = VMEM((pack_count(rows, False), 8, LANES), f32)
    pack_shape = VMEM((pack_count(rows, True), 8, LANES), f32)
    corner_shape = VMEM((3, 8, LANES), f32)
    edge_a, edge_b, inner, seas, gains, pack_a, pack_b = call(
        functools.partial(load_kernel, bins),
        (edge_shape, edge_shape, inner_shape, mask_shape, mask_shape, pack_shape, pack_own),
        (spectrum, sea_mask, ice_flags, wind_forcing), [vmem] * 4, flops=1 << 24,
    )
    stay, go_x, go_y, wide = call(
        functools.partial(table_kernel, bins, rows),
        (table_shape, table_shape, VMEM((8, padded), f32), VMEM((padded, padded), jnp.bfloat16)),
        (group_speed, jnp.asarray(angle_table(bins, group_speed.shape[0])), coupling),
        [smem, vmem, vmem], flops=1 << 24,
    )
    edge_b, seas, gains, corner_b = call(
        functools.partial(corner_kernel, bins), (edge_shape, mask_shape, mask_shape, corner_shape),
        (go_y, halo_a, halo_b, edge_b, seas, gains), [vmem] * 6, aliases={3: 0, 4: 1, 5: 2},
    )
    edge_a, inner, seas, gains, pack_a = call(
        functools.partial(join_kernel, bins), (edge_shape, inner_shape, mask_shape, mask_shape, pack_shape),
        (halo_a, halo_b, edge_a, inner, seas, gains, pack_a), [vmem] * 7,
        aliases={2: 0, 3: 1, 4: 2, 5: 3, 6: 4},
    )
    tables = (seas, gains, stay, go_x, go_y, wide)
    for step in range(STEPS):
        last = step == STEPS - 1
        halo_b = lax.ppermute(pack_b, "lon", lon_b)
        halo_a = lax.ppermute(pack_a, "lon", lon_a)
        if step == 0:
            corner = lax.ppermute(corner_b, "lon", lon_b)
        used = rows if last else tall
        new_inner = call(
            functools.partial(inner_kernel, bins), VMEM((columns - 2, rows, bins), f32) if last else inner_shape,
            (edge_a, edge_b, inner) + tables, [vmem] * 9,
            [VMEM(((columns - 2) * used, padded), f32), VMEM(((columns - 2) * used, padded), jnp.bfloat16),
             VMEM(((columns - 2) * used, LANES), f32)],
            flops=1 << 28,
        )
        if last:
            column = VMEM((rows, bins), f32)
            scratch = [VMEM((tall, padded), f32)]
            done_b = call(
                functools.partial(ordered_late_kernel, bins, True), column,
                (new_inner, halo_b, edge_b, inner) + tables, [vmem] * 10, scratch, flops=1 << 26,
            )
            return call(
                functools.partial(last_edge_kernel, bins, False), pltpu.HBM((columns, rows, bins), f32),
                (halo_a, edge_a, inner) + tables + (new_inner, done_b), [vmem] * 11,
                scratch + [column, pltpu.SemaphoreType.DMA((3,))], flops=1 << 26, out_specs=hbm,
            )
        fresh = []
        pack_next = VMEM((pack_count(rows, step < STEPS - 2), 8, LANES), f32)
        for second, halo, edge in ((False, halo_a, edge_a), (True, halo_b, edge_b)):
            body, ins = edge_kernel, (halo, edge, inner) + tables
            if step > 0:
                body, ins = ordered_edge_kernel, (new_inner,) + ins
            elif second:
                body, ins = ordered_first_kernel, (new_inner, corner) + ins
            fresh.append(call(
                functools.partial(body, bins, second), (edge_shape, pack_next),
                ins, [vmem] * len(ins), [VMEM((tall, padded), f32)], flops=1 << 26,
            ))
        inner = new_inner
        (edge_a, pack_a), (edge_b, pack_b) = fresh


def solution(mesh):
    placed = (P("lon", "lat", None), P("lon", "lat"), P("lon", "lat"), P("lon", "lat"), P(), P())
    return jax.shard_map(steps, mesh=mesh, in_specs=placed, out_specs=P("lon", "lat", None), check_vma=False)
```

profile of v0, /device:TPU:24, one launch (start us, length us, event | category | flops | bytes accessed | tf_op | source)
XLA Modules:
  0.0 37.1 jit_solution(13097105776638140320)
XLA Ops:
  0.0 0.0 copy-start
  0.0 0.0 copy-start.2
  0.0 0.0 copy-start.1
  0.0 0.0 copy-start.6
  0.1 1.3 %shard_map.73 = (f32[21,8,128]{2,1,0:T(8,128)S(1)}, f32[21,8,128]{2,1,0:T(8,128)S(1)}) custom-call(f32[8,64,648]{2,1,0:T(8,128)} %spectrum.3, s32[8,64]{1,0:T(8,128)} %sea_ref.1, s32[8,64]{1,0:T(8,128)} %ice_ref.1, f32[8,64]{1,0:T(8,128)} %wind_ref.1), custom_call_target="tpu_custom_call" | custom-call | tf_op jit(solution)/shard_map/pallas_call | solution.py:582
  1.4 0.1 collective-permute-start
  1.4 2.4 %collective-permute-start.1 = (f32[21,8,128]{2,1,0:T(8,128)S(1)}, f32[21,8,128]{2,1,0:T(8,128)S(1)}, u32[]{:S(2)}, u32[]{:S(2)}) collective-permute-start(f32[21,8,128]{2,1,0:T(8,128)S(1)} %get-tuple-element.40), channel_id=1, source_target_pairs={{1,2},{2,1},{3,4},{4,3},{5,6},{6,5},{9,10},{10,9},{11,12},{12,11},... | collective-permute-start | bytes 258056 | tf_op jit(solution)/shard_map/ppermute | solution.py:601
  3.9 0.0 copy-done.5
  3.9 0.0 copy-done.4
  3.9 0.0 copy-done.3
  3.9 0.0 copy-done
  3.9 0.7 %shard_map.74 = (f32[72,768]{1,0:T(8,128)S(1)}, f32[72,768]{1,0:T(8,128)S(1)}, f32[6,72,768]{2,1,0:T(8,128)S(1)}, f32[8,72,128]{2,1,0:T(8,128)S(1)}, f32[8,72,12...) custom-call(f32[8,64,648]{2,1,0:T(8,128)S(1)} %copy-done, s32[8,64]{1,0:T(8,128)S(1)} %copy-done.3, ...), custom_call_target="tpu_custom_call" | custom-call | flops 16777216 | tf_op jit(solution)/shard_map/pallas_call | solution.py:582
  4.6 0.0 copy-done.2
  4.6 0.8 %shard_map.75 = (f32[72,768]{1,0:T(8,128)S(1)}, f32[72,768]{1,0:T(8,128)S(1)}, f32[8,768]{1,0:T(8,128)S(1)}, bf16[768,768]{1,0:T(8,128)(2,1)S(1)}) custom-call(f32[18]{0:T(128)S(1)} %copy-done.6, f32[8,768]{1,0:T(8,128)S(1)} %copy-done.2, bf16[648,648]{1,0:T(8,128)(2,1)S(1)} %copy-done.1), custom_call_target="tpu_custom_call" | custom-call | flops 16777216 | tf_op jit(solution)/shard_map/pallas_call | solution.py:582
  5.4 0.0 collective-permute-done.halo_a
  5.5 1.8 %collective-permute-done.1.halo_b = f32[21,8,128]{2,1,0:T(8,128)S(1)} collective-permute-done((f32[21,8,128]{2,1,0:T(8,128)S(1)}, f32[21,8,128]{2,1,0:T(8,128)S(1)}, u32[]{:S(2)}, u32[]{:S(2)}) %collective-permute-start.1) | collective-permute-done | bytes 86048 | tf_op jit(solution)/shard_map/ppermute | solution.py:601
  7.2 0.1 shard_map.76
  7.3 0.4 shard_map.77
  7.7 1.5 %collective-permute-start.2 = (f32[23,8,128]{2,1,0:T(8,128)S(1)}, f32[23,8,128]{2,1,0:T(8,128)S(1)}, u32[]{:S(2)}, u32[]{:S(2)}) collective-permute-start(f32[23,8,128]{2,1,0:T(8,128)S(1)} %get-tuple-element.50), channel_id=1, source_target_pairs={{0,8},{8,0},{16,24},{24,16},{1,9},{9,1},{17,25},{25,17},{2,10},{10... | collective-permute-start | bytes 282632 | tf_op jit(solution)/shard_map/ppermute | solution.py:630
  9.2 1.6 %collective-permute-start.4 = (f32[21,8,128]{2,1,0:T(8,128)S(1)}, f32[21,8,128]{2,1,0:T(8,128)S(1)}, u32[]{:S(2)}, u32[]{:S(2)}) collective-permute-start(f32[21,8,128]{2,1,0:T(8,128)S(1)} %get-tuple-element.61), channel_id=1, source_target_pairs={{8,16},{16,8},{24,0},{0,24},{9,17},{17,9},{25,1},{1,25},{10,18},{1... | collective-permute-start | bytes 258056 | tf_op jit(solution)/shard_map/ppermute | solution.py:629
  10.7 1.4 %collective-permute-start.3 = (f32[3,8,128]{2,1,0:T(8,128)S(1)}, f32[3,8,128]{2,1,0:T(8,128)S(1)}, u32[]{:S(2)}, u32[]{:S(2)}) collective-permute-start(f32[3,8,128]{2,1,0:T(8,128)S(1)} %get-tuple-element.60), channel_id=1, source_target_pairs={{8,16},{16,8},{24,0},{0,24},{9,17},{17,9},{25,1},{1,25},{10,18},{1... | collective-permute-start | bytes 36872 | tf_op jit(solution)/shard_map/ppermute | solution.py:632
  12.1 1.0 %shard_map.79.after.inner.refs_2_ = f32[6,72,768]{2,1,0:T(8,128)S(1)} custom-call(f32[72,768]{1,0:T(8,128)S(1)} %get-tuple-element.51.edge.edge_a, f32[72,768]{1,0:T(8,128)S(1)} %get-tuple-element.59.edge_b.refs_1_, f32[6,72,768]{2,1,0:T(8,128)S(1)} %get-tuple-element.52.inner.refs_2_, f32[8,72,128]{2,1,0:T(8,128)S(1)} %get-tuple-element.53.seas.refs_3_, ...), custom_call_target="tpu_custom_call" | custom-call | flops 268435456 | tf_op jit(solution)/shard_map/pallas_call | solution.py:582
  13.1 1.5 %collective-permute-done.4.refs_0_ = f32[21,8,128]{2,1,0:T(8,128)S(1)} collective-permute-done((f32[21,8,128]{2,1,0:T(8,128)S(1)}, f32[21,8,128]{2,1,0:T(8,128)S(1)}, u32[]{:S(2)}, u32[]{:S(2)}) %collective-permute-start.4) | collective-permute-done | bytes 86048 | tf_op jit(solution)/shard_map/ppermute | solution.py:629
  14.6 0.9 %collective-permute-done.3.corner = f32[3,8,128]{2,1,0:T(8,128)S(1)} collective-permute-done((f32[3,8,128]{2,1,0:T(8,128)S(1)}, f32[3,8,128]{2,1,0:T(8,128)S(1)}, u32[]{:S(2)}, u32[]{:S(2)}) %collective-permute-start.3) | collective-permute-done | bytes 12320 | tf_op jit(solution)/shard_map/ppermute | solution.py:632
  15.5 0.5 %shard_map.80 = (f32[72,768]{1,0:T(8,128)S(1)}, f32[23,8,128]{2,1,0:T(8,128)S(1)}) custom-call(f32[6,72,768]{2,1,0:T(8,128)S(1)} %shard_map.79.after.inner.refs_2_, f32[3,8,128]{2,1,0:T(8,128)S(1)} %collective-permute-done.3.corner, f32[21,8,128]{2,1,0:T(8,128)S(1)} %collective-permute-done.4.refs_0_, f32[72,768]{1,0:T(8,128)S(1)} %get-tuple-element.59.edge_b.refs_1_, ...), custom_call_target="tpu_custom_call" | custom-call | flops 67108864 | tf_op jit(solution)/shard_map/pallas_call | solution.py:582
  15.9 1.4 %collective-permute-start.6 = (f32[23,8,128]{2,1,0:T(8,128)S(1)}, f32[23,8,128]{2,1,0:T(8,128)S(1)}, u32[]{:S(2)}, u32[]{:S(2)}) collective-permute-start(f32[23,8,128]{2,1,0:T(8,128)S(1)} %get-tuple-element.65), channel_id=1, source_target_pairs={{8,16},{16,8},{24,0},{0,24},{9,17},{17,9},{25,1},{1,25},{10,18},{1... | collective-permute-start | bytes 282632 | tf_op jit(solution)/shard_map/ppermute | solution.py:629
  17.4 0.0 collective-permute-done.2.halo
  17.4 0.5 %shard_map.78 = (f32[72,768]{1,0:T(8,128)S(1)}, f32[23,8,128]{2,1,0:T(8,128)S(1)}) custom-call(f32[23,8,128]{2,1,0:T(8,128)S(1)} %collective-permute-done.2.halo, f32[72,768]{1,0:T(8,128)S(1)} %get-tuple-element.51.edge.edge_a, f32[6,72,768]{2,1,0:T(8,128)S(1)} %get-tuple-element.52.inner.refs_2_, f32[8,72,128]{2,1,0:T(8,128)S(1)} %get-tuple-element.53.seas.refs_3_, ...), custom_call_target="tpu_custom_call" | custom-call | flops 67108864 | tf_op jit(solution)/shard_map/pallas_call | solution.py:582
  17.8 1.4 %collective-permute-start.5 = (f32[23,8,128]{2,1,0:T(8,128)S(1)}, f32[23,8,128]{2,1,0:T(8,128)S(1)}, u32[]{:S(2)}, u32[]{:S(2)}) collective-permute-start(f32[23,8,128]{2,1,0:T(8,128)S(1)} %get-tuple-element.63), channel_id=1, source_target_pairs={{0,8},{8,0},{16,24},{24,16},{1,9},{9,1},{17,25},{25,17},{2,10},{10... | collective-permute-start | bytes 282632 | tf_op jit(solution)/shard_map/ppermute | solution.py:630
  19.2 1.0 %shard_map.81.after.inner.refs_2_ = f32[6,72,768]{2,1,0:T(8,128)S(1)} custom-call(f32[72,768]{1,0:T(8,128)S(1)} %get-tuple-element.58.edge_a.refs_1_, f32[72,768]{1,0:T(8,128)S(1)} %get-tuple-element.62.edge_b.refs_1_, f32[6,72,768]{2,1,0:T(8,128)S(1)} %shard_map.79.after.inner.refs_2_, f32[8,72,128]{2,1,0:T(8,128)S(1)} %get-tuple-element.53.seas.refs_3_, ...), custom_call_target="tpu_custom_call" | custom-call | flops 268435456 | tf_op jit(solution)/shard_map/pallas_call | solution.py:582
  20.2 1.8 %collective-permute-done.6.refs_0_ = f32[23,8,128]{2,1,0:T(8,128)S(1)} collective-permute-done((f32[23,8,128]{2,1,0:T(8,128)S(1)}, f32[23,8,128]{2,1,0:T(8,128)S(1)}, u32[]{:S(2)}, u32[]{:S(2)}) %collective-permute-start.6) | collective-permute-done | bytes 94240 | tf_op jit(solution)/shard_map/ppermute | solution.py:629
  22.0 0.5 %shard_map.83 = (f32[72,768]{1,0:T(8,128)S(1)}, f32[23,8,128]{2,1,0:T(8,128)S(1)}) custom-call(f32[6,72,768]{2,1,0:T(8,128)S(1)} %shard_map.81.after.inner.refs_2_, f32[23,8,128]{2,1,0:T(8,128)S(1)} %collective-permute-done.6.refs_0_, f32[72,768]{1,0:T(8,128)S(1)} %get-tuple-element.62.edge_b.refs_1_, f32[6,72,768]{2,1,0:T(8,128)S(1)} %shard_map.79.after.inner.refs_2_, ...), custom_call_target="tpu_custom_call" | custom-call | flops 67108864 | tf_op jit(solution)/shard_map/pallas_call | solution.py:582
  22.5 1.5 %collective-permute-start.9 = (f32[23,8,128]{2,1,0:T(8,128)S(1)}, f32[23,8,128]{2,1,0:T(8,128)S(1)}, u32[]{:S(2)}, u32[]{:S(2)}) collective-permute-start(f32[23,8,128]{2,1,0:T(8,128)S(1)} %get-tuple-element.70), channel_id=1, source_target_pairs={{8,16},{16,8},{24,0},{0,24},{9,17},{17,9},{25,1},{1,25},{10,18},{1... | collective-permute-start | bytes 282632 | tf_op jit(solution)/shard_map/ppermute | solution.py:629
  24.0 0.0 collective-permute-done.5.refs_0_
  24.0 0.5 %shard_map.82 = (f32[72,768]{1,0:T(8,128)S(1)}, f32[23,8,128]{2,1,0:T(8,128)S(1)}) custom-call(f32[6,72,768]{2,1,0:T(8,128)S(1)} %shard_map.81.after.inner.refs_2_, f32[23,8,128]{2,1,0:T(8,128)S(1)} %collective-permute-done.5.refs_0_, f32[72,768]{1,0:T(8,128)S(1)} %get-tuple-element.58.edge_a.refs_1_, f32[6,72,768]{2,1,0:T(8,128)S(1)} %shard_map.79.after.inner.refs_2_, ...), custom_call_target="tpu_custom_call" | custom-call | flops 67108864 | tf_op jit(solution)/shard_map/pallas_call | solution.py:582
  24.5 1.8 %collective-permute-start.7 = (f32[23,8,128]{2,1,0:T(8,128)S(1)}, f32[23,8,128]{2,1,0:T(8,128)S(1)}, u32[]{:S(2)}, u32[]{:S(2)}) collective-permute-start(f32[23,8,128]{2,1,0:T(8,128)S(1)} %get-tuple-element.67), channel_id=1, source_target_pairs={{0,8},{8,0},{16,24},{24,16},{1,9},{9,1},{17,25},{25,17},{2,10},{10... | collective-permute-start | bytes 282632 | tf_op jit(solution)/shard_map/ppermute | solution.py:630
  26.3 1.0 %shard_map.84.after.inner.refs_2_ = f32[6,72,768]{2,1,0:T(8,128)S(1)} custom-call(f32[72,768]{1,0:T(8,128)S(1)} %get-tuple-element.64.edge_a.refs_1_, f32[72,768]{1,0:T(8,128)S(1)} %get-tuple-element.66.edge_b.refs_1_, f32[6,72,768]{2,1,0:T(8,128)S(1)} %shard_map.81.after.inner.refs_2_, f32[8,72,128]{2,1,0:T(8,128)S(1)} %get-tuple-element.53.seas.refs_3_, ...), custom_call_target="tpu_custom_call" | custom-call | flops 268435456 | tf_op jit(solution)/shard_map/pallas_call | solution.py:582
  27.3 1.3 %collective-permute-done.9.refs_0_ = f32[23,8,128]{2,1,0:T(8,128)S(1)} collective-permute-done((f32[23,8,128]{2,1,0:T(8,128)S(1)}, f32[23,8,128]{2,1,0:T(8,128)S(1)}, u32[]{:S(2)}, u32[]{:S(2)}) %collective-permute-start.9) | collective-permute-done | bytes 94240 | tf_op jit(solution)/shard_map/ppermute | solution.py:629
  28.6 0.5 %shard_map.86 = (f32[72,768]{1,0:T(8,128)S(1)}, f32[21,8,128]{2,1,0:T(8,128)S(1)}) custom-call(f32[6,72,768]{2,1,0:T(8,128)S(1)} %shard_map.84.after.inner.refs_2_, f32[23,8,128]{2,1,0:T(8,128)S(1)} %collective-permute-done.9.refs_0_, f32[72,768]{1,0:T(8,128)S(1)} %get-tuple-element.66.edge_b.refs_1_, f32[6,72,768]{2,1,0:T(8,128)S(1)} %shard_map.81.after.inner.refs_2_, ...), custom_call_target="tpu_custom_call" | custom-call | flops 67108864 | tf_op jit(solution)/shard_map/pallas_call | solution.py:582
  29.0 1.8 %collective-permute-start.10 = (f32[21,8,128]{2,1,0:T(8,128)S(1)}, f32[21,8,128]{2,1,0:T(8,128)S(1)}, u32[]{:S(2)}, u32[]{:S(2)}) collective-permute-start(f32[21,8,128]{2,1,0:T(8,128)S(1)} %get-tuple-element.72), channel_id=1, source_target_pairs={{8,16},{16,8},{24,0},{0,24},{9,17},{17,9},{25,1},{1,25},{10,18},{1... | collective-permute-start | bytes 258056 | tf_op jit(solution)/shard_map/ppermute | solution.py:629
  30.9 0.0 collective-permute-done.7.refs_0_
  30.9 0.5 %shard_map.85 = (f32[72,768]{1,0:T(8,128)S(1)}, f32[21,8,128]{2,1,0:T(8,128)S(1)}) custom-call(f32[6,72,768]{2,1,0:T(8,128)S(1)} %shard_map.84.after.inner.refs_2_, f32[23,8,128]{2,1,0:T(8,128)S(1)} %collective-permute-done.7.refs_0_, f32[72,768]{1,0:T(8,128)S(1)} %get-tuple-element.64.edge_a.refs_1_, f32[6,72,768]{2,1,0:T(8,128)S(1)} %shard_map.81.after.inner.refs_2_, ...), custom_call_target="tpu_custom_call" | custom-call | flops 67108864 | tf_op jit(solution)/shard_map/pallas_call | solution.py:582
  31.4 0.9 %collective-permute-start.8 = (f32[21,8,128]{2,1,0:T(8,128)S(1)}, f32[21,8,128]{2,1,0:T(8,128)S(1)}, u32[]{:S(2)}, u32[]{:S(2)}) collective-permute-start(f32[21,8,128]{2,1,0:T(8,128)S(1)} %get-tuple-element.68), channel_id=1, source_target_pairs={{0,8},{8,0},{16,24},{24,16},{1,9},{9,1},{17,25},{25,17},{2,10},{10... | collective-permute-start | bytes 258056 | tf_op jit(solution)/shard_map/ppermute | solution.py:630
  32.3 0.9 %shard_map.87.after.done_inner = f32[6,64,648]{2,1,0:T(8,128)S(1)} custom-call(f32[72,768]{1,0:T(8,128)S(1)} %get-tuple-element.69.edge_a.edge, f32[72,768]{1,0:T(8,128)S(1)} %get-tuple-element.71.edge_b.refs_1_, f32[6,72,768]{2,1,0:T(8,128)S(1)} %shard_map.84.after.inner.refs_2_, f32[8,72,128]{2,1,0:T(8,128)S(1)} %get-tuple-element.53.seas.refs_3_, ...), custom_call_target="tpu_custom_call" | custom-call | flops 268435456 | tf_op jit(solution)/shard_map/pallas_call | solution.py:582
  33.2 1.3 %collective-permute-done.10.refs_0_ = f32[21,8,128]{2,1,0:T(8,128)S(1)} collective-permute-done((f32[21,8,128]{2,1,0:T(8,128)S(1)}, f32[21,8,128]{2,1,0:T(8,128)S(1)}, u32[]{:S(2)}, u32[]{:S(2)}) %collective-permute-start.10) | collective-permute-done | bytes 86048 | tf_op jit(solution)/shard_map/ppermute | solution.py:629
  34.5 0.4 %shard_map.88.done_edge = f32[64,648]{1,0:T(8,128)S(1)} custom-call(f32[6,64,648]{2,1,0:T(8,128)S(1)} %shard_map.87.after.done_inner, f32[21,8,128]{2,1,0:T(8,128)S(1)} %collective-permute-done.10.refs_0_, f32[72,768]{1,0:T(8,128)S(1)} %get-tuple-element.71.edge_b.refs_1_, f32[6,72,768]{2,1,0:T(8,128)S(1)} %shard_map.84.after.inner.refs_2_, ...), custom_call_target="tpu_custom_call" | custom-call | flops 67108864 | tf_op jit(solution)/shard_map/pallas_call | solution.py:582
  34.9 1.0 %collective-permute-done.8.halo = f32[21,8,128]{2,1,0:T(8,128)S(1)} collective-permute-done((f32[21,8,128]{2,1,0:T(8,128)S(1)}, f32[21,8,128]{2,1,0:T(8,128)S(1)}, u32[]{:S(2)}, u32[]{:S(2)}) %collective-permute-start.8) | collective-permute-done | bytes 86048 | tf_op jit(solution)/shard_map/ppermute | solution.py:630
  35.9 1.2 %shard_map.89 = f32[8,64,648]{2,1,0:T(8,128)} custom-call(f32[21,8,128]{2,1,0:T(8,128)S(1)} %collective-permute-done.8.halo, f32[72,768]{1,0:T(8,128)S(1)} %get-tuple-element.69.edge_a.edge, f32[6,72,768]{2,1,0:T(8,128)S(1)} %shard_map.84.after.inner.refs_2_, f32[8,72,128]{2,1,0:T(8,128)S(1)} %get-tuple-element.53.seas.refs_3_, ...), custom_call_target="tpu_custom_call" | custom-call | flops 67108864 | tf_op jit(solution)/shard_map/pallas_call | solution.py:582
  (5 shorter events, 0.0 us)
Async XLA Ops:
  0.0 3.9 %copy-start.5 = (f32[8,64]{1,0:T(8,128)S(1)}, f32[8,64]{1,0:T(8,128)}, u32[]{:S(2)}) copy-start(f32[8,64]{1,0:T(8,128)} %wind_ref.1) | copy-start | bytes 6148
  0.0 3.9 %copy-start.4 = (s32[8,64]{1,0:T(8,128)S(1)}, s32[8,64]{1,0:T(8,128)}, u32[]{:S(2)}) copy-start(s32[8,64]{1,0:T(8,128)} %ice_ref.1) | copy-start | bytes 6148
  0.0 3.9 %copy-start.3 = (s32[8,64]{1,0:T(8,128)S(1)}, s32[8,64]{1,0:T(8,128)}, u32[]{:S(2)}) copy-start(s32[8,64]{1,0:T(8,128)} %sea_ref.1) | copy-start | bytes 6148
  0.0 3.9 %copy-start = (f32[8,64,648]{2,1,0:T(8,128)S(1)}, f32[8,64,648]{2,1,0:T(8,128)}, u32[]{:S(2)}) copy-start(f32[8,64,648]{2,1,0:T(8,128)} %spectrum.3) | copy-start | bytes 3981316
  0.0 4.6 %copy-start.2 = (f32[8,768]{1,0:T(8,128)S(1)}, f32[8,768]{1,0:T(8,128)}, u32[]{:S(2)}) copy-start(f32[8,768]{1,0:T(8,128)} %constant.2.clone.angle_ref) | copy-start | bytes 73732
  0.0 4.6 %copy-start.1 = (bf16[648,648]{1,0:T(8,128)(2,1)S(1)}, bf16[648,648]{1,0:T(8,128)(2,1)}, u32[]{:S(2)}) copy-start(bf16[648,648]{1,0:T(8,128)(2,1)} %coupling_ref.1) | copy-start | bytes 2519428
  0.0 4.6 %copy-start.6 = (f32[18]{0:T(128)S(1)}, f32[18]{0:T(128)}, u32[]{:S(2)}) copy-start(f32[18]{0:T(128)} %speed_ref.1) | copy-start | bytes 220
  1.4 4.1 %collective-permute-start = (f32[21,8,128]{2,1,0:T(8,128)S(1)}, f32[21,8,128]{2,1,0:T(8,128)S(1)}, u32[]{:S(2)}, u32[]{:S(2)}) collective-permute-start(f32[21,8,128]{2,1,0:T(8,128)S(1)} %get-tuple-element.39), channel_id=1, source_target_pairs={{0,1},{1,0},{2,3},{3,2},{4,5},{5,4},{6,7},{7,6},{8,9},{9,8},{10,11... | collective-permute-start | bytes 258056 | tf_op jit(solution)/shard_map/ppermute | solution.py:602
  1.4 5.8 %collective-permute-start.1 = (f32[21,8,128]{2,1,0:T(8,128)S(1)}, f32[21,8,128]{2,1,0:T(8,128)S(1)}, u32[]{:S(2)}, u32[]{:S(2)}) collective-permute-start(f32[21,8,128]{2,1,0:T(8,128)S(1)} %get-tuple-element.40), channel_id=1, source_target_pairs={{1,2},{2,1},{3,4},{4,3},{5,6},{6,5},{9,10},{10,9},{11,12},{12,11},... | collective-permute-start | bytes 258056 | tf_op jit(solution)/shard_map/ppermute | solution.py:601
  7.7 9.7 %collective-permute-start.2 = (f32[23,8,128]{2,1,0:T(8,128)S(1)}, f32[23,8,128]{2,1,0:T(8,128)S(1)}, u32[]{:S(2)}, u32[]{:S(2)}) collective-permute-start(f32[23,8,128]{2,1,0:T(8,128)S(1)} %get-tuple-element.50), channel_id=1, source_target_pairs={{0,8},{8,0},{16,24},{24,16},{1,9},{9,1},{17,25},{25,17},{2,10},{10... | collective-permute-start | bytes 282632 | tf_op jit(solution)/shard_map/ppermute | solution.py:630
  9.2 5.4 %collective-permute-start.4 = (f32[21,8,128]{2,1,0:T(8,128)S(1)}, f32[21,8,128]{2,1,0:T(8,128)S(1)}, u32[]{:S(2)}, u32[]{:S(2)}) collective-permute-start(f32[21,8,128]{2,1,0:T(8,128)S(1)} %get-tuple-element.61), channel_id=1, source_target_pairs={{8,16},{16,8},{24,0},{0,24},{9,17},{17,9},{25,1},{1,25},{10,18},{1... | collective-permute-start | bytes 258056 | tf_op jit(solution)/shard_map/ppermute | solution.py:629
  10.7 4.7 %collective-permute-start.3 = (f32[3,8,128]{2,1,0:T(8,128)S(1)}, f32[3,8,128]{2,1,0:T(8,128)S(1)}, u32[]{:S(2)}, u32[]{:S(2)}) collective-permute-start(f32[3,8,128]{2,1,0:T(8,128)S(1)} %get-tuple-element.60), channel_id=1, source_target_pairs={{8,16},{16,8},{24,0},{0,24},{9,17},{17,9},{25,1},{1,25},{10,18},{1... | collective-permute-start | bytes 36872 | tf_op jit(solution)/shard_map/ppermute | solution.py:632
  15.9 6.1 %collective-permute-start.6 = (f32[23,8,128]{2,1,0:T(8,128)S(1)}, f32[23,8,128]{2,1,0:T(8,128)S(1)}, u32[]{:S(2)}, u32[]{:S(2)}) collective-permute-start(f32[23,8,128]{2,1,0:T(8,128)S(1)} %get-tuple-element.65), channel_id=1, source_target_pairs={{8,16},{16,8},{24,0},{0,24},{9,17},{17,9},{25,1},{1,25},{10,18},{1... | collective-permute-start | bytes 282632 | tf_op jit(solution)/shard_map/ppermute | solution.py:629
  17.8 6.2 %collective-permute-start.5 = (f32[23,8,128]{2,1,0:T(8,128)S(1)}, f32[23,8,128]{2,1,0:T(8,128)S(1)}, u32[]{:S(2)}, u32[]{:S(2)}) collective-permute-start(f32[23,8,128]{2,1,0:T(8,128)S(1)} %get-tuple-element.63), channel_id=1, source_target_pairs={{0,8},{8,0},{16,24},{24,16},{1,9},{9,1},{17,25},{25,17},{2,10},{10... | collective-permute-start | bytes 282632 | tf_op jit(solution)/shard_map/ppermute | solution.py:630
  22.5 6.1 %collective-permute-start.9 = (f32[23,8,128]{2,1,0:T(8,128)S(1)}, f32[23,8,128]{2,1,0:T(8,128)S(1)}, u32[]{:S(2)}, u32[]{:S(2)}) collective-permute-start(f32[23,8,128]{2,1,0:T(8,128)S(1)} %get-tuple-element.70), channel_id=1, source_target_pairs={{8,16},{16,8},{24,0},{0,24},{9,17},{17,9},{25,1},{1,25},{10,18},{1... | collective-permute-start | bytes 282632 | tf_op jit(solution)/shard_map/ppermute | solution.py:629
  24.5 6.4 %collective-permute-start.7 = (f32[23,8,128]{2,1,0:T(8,128)S(1)}, f32[23,8,128]{2,1,0:T(8,128)S(1)}, u32[]{:S(2)}, u32[]{:S(2)}) collective-permute-start(f32[23,8,128]{2,1,0:T(8,128)S(1)} %get-tuple-element.67), channel_id=1, source_target_pairs={{0,8},{8,0},{16,24},{24,16},{1,9},{9,1},{17,25},{25,17},{2,10},{10... | collective-permute-start | bytes 282632 | tf_op jit(solution)/shard_map/ppermute | solution.py:630
  29.0 5.5 %collective-permute-start.10 = (f32[21,8,128]{2,1,0:T(8,128)S(1)}, f32[21,8,128]{2,1,0:T(8,128)S(1)}, u32[]{:S(2)}, u32[]{:S(2)}) collective-permute-start(f32[21,8,128]{2,1,0:T(8,128)S(1)} %get-tuple-element.72), channel_id=1, source_target_pairs={{8,16},{16,8},{24,0},{0,24},{9,17},{17,9},{25,1},{1,25},{10,18},{1... | collective-permute-start | bytes 258056 | tf_op jit(solution)/shard_map/ppermute | solution.py:629
  31.4 4.6 %collective-permute-start.8 = (f32[21,8,128]{2,1,0:T(8,128)S(1)}, f32[21,8,128]{2,1,0:T(8,128)S(1)}, u32[]{:S(2)}, u32[]{:S(2)}) collective-permute-start(f32[21,8,128]{2,1,0:T(8,128)S(1)} %get-tuple-element.68), channel_id=1, source_target_pairs={{0,8},{8,0},{16,24},{24,16},{1,9},{9,1},{17,25},{25,17},{2,10},{10... | collective-permute-start | bytes 258056 | tf_op jit(solution)/shard_map/ppermute | solution.py:630
where the time goes:
time: 37.2 us; the launch traced here: 37.1 us
  starting transfers between devices  15.8 us (42%)
  Pallas kernels  11.5 us (31%)
  waiting for transfers between devices  9.5 us (26%)
    pallas_call x17, Pallas kernels, call(): pl.pallas_call(body, out_shape=outs, in_specs=specs, out_specs=out_specs...  11.5 us
    ppermute x4, starting transfers between devices, steps(): halo_b = lax.ppermute(pack_b, 'lon', lon_b)  6.33 us
    ppermute x4, waiting for transfers between devices, steps(): halo_b = lax.ppermute(pack_b, 'lon', lon_b)  5.8 us
    ppermute x4, starting transfers between devices, steps(): halo_a = lax.ppermute(pack_a, 'lon', lon_a)  5.57 us
    ppermute x1, starting transfers between devices, steps(): halo_b = lax.ppermute(send_b, 'lat', lat_b)  2.45 us
    ppermute x1, waiting for transfers between devices, steps(): halo_b = lax.ppermute(send_b, 'lat', lat_b)  1.78 us
    ppermute x1, starting transfers between devices, steps(): corner = lax.ppermute(corner_b, 'lon', lon_b)  1.37 us
    ppermute x4, waiting for transfers between devices, steps(): halo_a = lax.ppermute(pack_a, 'lon', lon_a)  1.02 us
  transfers between devices with their start and end apart: 11, of which 7 were waited for; matrix products, arithmetic and copies ran while one was open for 0% of the time, Pallas kernels for 23%

commit v1 on v0

--- a/solution.py
+++ b/solution.py
@@ -139,8 +139,9 @@
                 left = jnp.where((lane >= low) & (lane < low + rest), turn(part, low - kept - start), left)
         else:
             left = jnp.where(lane >= half * rest, turn(part, half * rest - start), left)
-            out[2 * blocks + half + 1] = full
-            out[2 * blocks + half + 2] = other
+            row = row_index((8, LANES))
+            near = (row < 2) | (row >= 6)
+            out[2 * blocks + half + 1] = jnp.where(near, full, pltpu.roll(other, 4, 0))
     out[2 * blocks + half] = left
 
 
@@ -171,7 +172,11 @@
             if block == blocks and corner is not None:
                 full, other, part = corner[0], corner[1], corner[2]
             elif block == blocks:
-                full, other = halo[2 * blocks + half + 1], halo[2 * blocks + half + 2]
+                full = halo[2 * blocks + half + 1]
+                if halo.shape[0] > 2 * blocks + half + 2:
+                    other = halo[2 * blocks + half + 2]
+                else:
+                    other = pltpu.roll(full, 4, 0)
                 part = turn(left, start - half * rest)
             else:
                 full, other = halo[block], halo[blocks + block]
@@ -431,7 +436,7 @@
     bins, second, halo, edge, inner, seas, gains, stay, go_x, go_y, wide, out, pack, adv_ref, corner=None
 ):
     rows = edge.shape[0] - 2 * DEPTH
-    halo_next = pack.shape[0] == pack_count(rows, True)
+    halo_next = pack.shape[0] > pack_count(rows, False)
 
     def side(west):
         fresh = edge_step(bins, west, halo, edge, inner, seas, gains, stay, go_x, go_y, wide, adv_ref, False, corner)
@@ -507,7 +512,7 @@
     count, tall = inner.shape[0], inner.shape[1]
     rows = adv_ref.shape[0] // count
     a_west = west_flag(False)
-    parts = 2
+    parts = 1
     if count % parts:
         parts = 1
     for part in range(parts):
@@ -651,7 +656,7 @@
                 scratch + [column, pltpu.SemaphoreType.DMA((3,))], flops=1 << 26, out_specs=hbm,
             )
         fresh = []
-        pack_next = VMEM((pack_count(rows, step < STEPS - 2), 8, LANES), f32)
+        pack_next = VMEM((pack_count(rows, False) + (1 if step < STEPS - 2 else 0), 8, LANES), f32)
         for second, halo, edge in ((False, halo_a, edge_a), (True, halo_b, edge_b)):
             body, ins = edge_kernel, (halo, edge, inner) + tables
             if step > 0:

time: 37.2 us -> 37 us (level)
  no operation moved by 1% of the time
where the time goes in v1:
time: 37 us; the launch traced here: 36.8 us
  starting transfers between devices  15.9 us (43%)
  Pallas kernels  11.4 us (31%)
  waiting for transfers between devices  9.17 us (25%)
    pallas_call x17, Pallas kernels, call(): pl.pallas_call(body, out_shape=outs, in_specs=specs, out_specs=out_specs...  11.4 us
    ppermute x4, starting transfers between devices, steps(): halo_b = lax.ppermute(pack_b, 'lon', lon_b)  6.23 us
    ppermute x4, starting transfers between devices, steps(): halo_a = lax.ppermute(pack_a, 'lon', lon_a)  5.8 us
    ppermute x4, waiting for transfers between devices, steps(): halo_b = lax.ppermute(pack_b, 'lon', lon_b)  5.58 us
    ppermute x1, starting transfers between devices, steps(): halo_b = lax.ppermute(send_b, 'lat', lat_b)  2.45 us
    ppermute x1, waiting for transfers between devices, steps(): halo_b = lax.ppermute(send_b, 'lat', lat_b)  1.77 us
    ppermute x1, starting transfers between devices, steps(): corner = lax.ppermute(corner_b, 'lon', lon_b)  1.37 us
    ppermute x4, waiting for transfers between devices, steps(): halo_a = lax.ppermute(pack_a, 'lon', lon_a)  0.92 us
  transfers between devices with their start and end apart: 11, of which 7 were waited for; matrix products, arithmetic and copies ran while one was open for 0% of the time, Pallas kernels for 23%

profile of v1, /device:TPU:24, one launch (start us, length us, event | category | flops | bytes accessed | tf_op | source)
XLA Modules:
  0.0 36.8 jit_solution(3818359330811360663)
XLA Ops:
  0.0 0.0 copy-start
  0.0 0.0 copy-start.2
  0.0 0.0 copy-start.1
  0.0 0.0 copy-start.6
  0.1 1.3 %shard_map.73 = (f32[21,8,128]{2,1,0:T(8,128)S(1)}, f32[21,8,128]{2,1,0:T(8,128)S(1)}) custom-call(f32[8,64,648]{2,1,0:T(8,128)} %spectrum.3, s32[8,64]{1,0:T(8,128)} %sea_ref.1, s32[8,64]{1,0:T(8,128)} %ice_ref.1, f32[8,64]{1,0:T(8,128)} %wind_ref.1), custom_call_target="tpu_custom_call" | custom-call | tf_op jit(solution)/shard_map/pallas_call | solution.py:587
  1.4 0.1 collective-permute-start
  1.4 2.4 %collective-permute-start.1 = (f32[21,8,128]{2,1,0:T(8,128)S(1)}, f32[21,8,128]{2,1,0:T(8,128)S(1)}, u32[]{:S(2)}, u32[]{:S(2)}) collective-permute-start(f32[21,8,128]{2,1,0:T(8,128)S(1)} %get-tuple-element.40), channel_id=1, source_target_pairs={{1,2},{2,1},{3,4},{4,3},{5,6},{6,5},{9,10},{10,9},{11,12},{12,11},... | collective-permute-start | bytes 258056 | tf_op jit(solution)/shard_map/ppermute | solution.py:606
  3.9 0.0 copy-done.5
  3.9 0.0 copy-done.4
  3.9 0.0 copy-done.3
  3.9 0.0 copy-done
  3.9 0.7 %shard_map.74 = (f32[72,768]{1,0:T(8,128)S(1)}, f32[72,768]{1,0:T(8,128)S(1)}, f32[6,72,768]{2,1,0:T(8,128)S(1)}, f32[8,72,128]{2,1,0:T(8,128)S(1)}, f32[8,72,12...) custom-call(f32[8,64,648]{2,1,0:T(8,128)S(1)} %copy-done, s32[8,64]{1,0:T(8,128)S(1)} %copy-done.3, ...), custom_call_target="tpu_custom_call" | custom-call | flops 16777216 | tf_op jit(solution)/shard_map/pallas_call | solution.py:587
  4.6 0.0 copy-done.2
  4.6 0.8 %shard_map.75 = (f32[72,768]{1,0:T(8,128)S(1)}, f32[72,768]{1,0:T(8,128)S(1)}, f32[8,768]{1,0:T(8,128)S(1)}, bf16[768,768]{1,0:T(8,128)(2,1)S(1)}) custom-call(f32[18]{0:T(128)S(1)} %copy-done.6, f32[8,768]{1,0:T(8,128)S(1)} %copy-done.2, bf16[648,648]{1,0:T(8,128)(2,1)S(1)} %copy-done.1), custom_call_target="tpu_custom_call" | custom-call | flops 16777216 | tf_op jit(solution)/shard_map/pallas_call | solution.py:587
  5.4 0.0 collective-permute-done.halo_a
  5.5 1.8 %collective-permute-done.1.halo_b = f32[21,8,128]{2,1,0:T(8,128)S(1)} collective-permute-done((f32[21,8,128]{2,1,0:T(8,128)S(1)}, f32[21,8,128]{2,1,0:T(8,128)S(1)}, u32[]{:S(2)}, u32[]{:S(2)}) %collective-permute-start.1) | collective-permute-done | bytes 86048 | tf_op jit(solution)/shard_map/ppermute | solution.py:606
  7.2 0.1 shard_map.76
  7.3 0.4 shard_map.77
  7.7 1.5 %collective-permute-start.2 = (f32[23,8,128]{2,1,0:T(8,128)S(1)}, f32[23,8,128]{2,1,0:T(8,128)S(1)}, u32[]{:S(2)}, u32[]{:S(2)}) collective-permute-start(f32[23,8,128]{2,1,0:T(8,128)S(1)} %get-tuple-element.50), channel_id=1, source_target_pairs={{0,8},{8,0},{16,24},{24,16},{1,9},{9,1},{17,25},{25,17},{2,10},{10... | collective-permute-start | bytes 282632 | tf_op jit(solution)/shard_map/ppermute | solution.py:635
  9.2 1.6 %collective-permute-start.4 = (f32[21,8,128]{2,1,0:T(8,128)S(1)}, f32[21,8,128]{2,1,0:T(8,128)S(1)}, u32[]{:S(2)}, u32[]{:S(2)}) collective-permute-start(f32[21,8,128]{2,1,0:T(8,128)S(1)} %get-tuple-element.61), channel_id=1, source_target_pairs={{8,16},{16,8},{24,0},{0,24},{9,17},{17,9},{25,1},{1,25},{10,18},{1... | collective-permute-start | bytes 258056 | tf_op jit(solution)/shard_map/ppermute | solution.py:634
  10.7 1.4 %collective-permute-start.3 = (f32[3,8,128]{2,1,0:T(8,128)S(1)}, f32[3,8,128]{2,1,0:T(8,128)S(1)}, u32[]{:S(2)}, u32[]{:S(2)}) collective-permute-start(f32[3,8,128]{2,1,0:T(8,128)S(1)} %get-tuple-element.60), channel_id=1, source_target_pairs={{8,16},{16,8},{24,0},{0,24},{9,17},{17,9},{25,1},{1,25},{10,18},{1... | collective-permute-start | bytes 36872 | tf_op jit(solution)/shard_map/ppermute | solution.py:637
  12.1 1.0 %shard_map.79.after.inner.refs_2_ = f32[6,72,768]{2,1,0:T(8,128)S(1)} custom-call(f32[72,768]{1,0:T(8,128)S(1)} %get-tuple-element.51.edge.edge_a, f32[72,768]{1,0:T(8,128)S(1)} %get-tuple-element.59.edge_b.refs_1_, f32[6,72,768]{2,1,0:T(8,128)S(1)} %get-tuple-element.52.inner.refs_2_, f32[8,72,128]{2,1,0:T(8,128)S(1)} %get-tuple-element.53.seas.refs_3_, ...), custom_call_target="tpu_custom_call" | custom-call | flops 268435456 | tf_op jit(solution)/shard_map/pallas_call | solution.py:587
  13.1 1.5 %collective-permute-done.4.refs_0_ = f32[21,8,128]{2,1,0:T(8,128)S(1)} collective-permute-done((f32[21,8,128]{2,1,0:T(8,128)S(1)}, f32[21,8,128]{2,1,0:T(8,128)S(1)}, u32[]{:S(2)}, u32[]{:S(2)}) %collective-permute-start.4) | collective-permute-done | bytes 86048 | tf_op jit(solution)/shard_map/ppermute | solution.py:634
  14.6 0.9 %collective-permute-done.3.corner = f32[3,8,128]{2,1,0:T(8,128)S(1)} collective-permute-done((f32[3,8,128]{2,1,0:T(8,128)S(1)}, f32[3,8,128]{2,1,0:T(8,128)S(1)}, u32[]{:S(2)}, u32[]{:S(2)}) %collective-permute-start.3) | collective-permute-done | bytes 12320 | tf_op jit(solution)/shard_map/ppermute | solution.py:637
  15.5 0.5 %shard_map.80 = (f32[72,768]{1,0:T(8,128)S(1)}, f32[22,8,128]{2,1,0:T(8,128)S(1)}) custom-call(f32[6,72,768]{2,1,0:T(8,128)S(1)} %shard_map.79.after.inner.refs_2_, f32[3,8,128]{2,1,0:T(8,128)S(1)} %collective-permute-done.3.corner, f32[21,8,128]{2,1,0:T(8,128)S(1)} %collective-permute-done.4.refs_0_, f32[72,768]{1,0:T(8,128)S(1)} %get-tuple-element.59.edge_b.refs_1_, ...), custom_call_target="tpu_custom_call" | custom-call | flops 67108864 | tf_op jit(solution)/shard_map/pallas_call | solution.py:587
  15.9 1.4 %collective-permute-start.6 = (f32[22,8,128]{2,1,0:T(8,128)S(1)}, f32[22,8,128]{2,1,0:T(8,128)S(1)}, u32[]{:S(2)}, u32[]{:S(2)}) collective-permute-start(f32[22,8,128]{2,1,0:T(8,128)S(1)} %get-tuple-element.65), channel_id=1, source_target_pairs={{8,16},{16,8},{24,0},{0,24},{9,17},{17,9},{25,1},{1,25},{10,18},{1... | collective-permute-start | bytes 270344 | tf_op jit(solution)/shard_map/ppermute | solution.py:634
  17.4 0.0 collective-permute-done.2.halo
  17.4 0.5 %shard_map.78 = (f32[72,768]{1,0:T(8,128)S(1)}, f32[22,8,128]{2,1,0:T(8,128)S(1)}) custom-call(f32[23,8,128]{2,1,0:T(8,128)S(1)} %collective-permute-done.2.halo, f32[72,768]{1,0:T(8,128)S(1)} %get-tuple-element.51.edge.edge_a, f32[6,72,768]{2,1,0:T(8,128)S(1)} %get-tuple-element.52.inner.refs_2_, f32[8,72,128]{2,1,0:T(8,128)S(1)} %get-tuple-element.53.seas.refs_3_, ...), custom_call_target="tpu_custom_call" | custom-call | flops 67108864 | tf_op jit(solution)/shard_map/pallas_call | solution.py:587
  17.8 1.4 %collective-permute-start.5 = (f32[22,8,128]{2,1,0:T(8,128)S(1)}, f32[22,8,128]{2,1,0:T(8,128)S(1)}, u32[]{:S(2)}, u32[]{:S(2)}) collective-permute-start(f32[22,8,128]{2,1,0:T(8,128)S(1)} %get-tuple-element.63), channel_id=1, source_target_pairs={{0,8},{8,0},{16,24},{24,16},{1,9},{9,1},{17,25},{25,17},{2,10},{10... | collective-permute-start | bytes 270344 | tf_op jit(solution)/shard_map/ppermute | solution.py:635
  19.2 1.0 %shard_map.81.after.inner.refs_2_ = f32[6,72,768]{2,1,0:T(8,128)S(1)} custom-call(f32[72,768]{1,0:T(8,128)S(1)} %get-tuple-element.58.edge_a.refs_1_, f32[72,768]{1,0:T(8,128)S(1)} %get-tuple-element.62.edge_b.refs_1_, f32[6,72,768]{2,1,0:T(8,128)S(1)} %shard_map.79.after.inner.refs_2_, f32[8,72,128]{2,1,0:T(8,128)S(1)} %get-tuple-element.53.seas.refs_3_, ...), custom_call_target="tpu_custom_call" | custom-call | flops 268435456 | tf_op jit(solution)/shard_map/pallas_call | solution.py:587
  20.2 1.6 %collective-permute-done.6.refs_0_ = f32[22,8,128]{2,1,0:T(8,128)S(1)} collective-permute-done((f32[22,8,128]{2,1,0:T(8,128)S(1)}, f32[22,8,128]{2,1,0:T(8,128)S(1)}, u32[]{:S(2)}, u32[]{:S(2)}) %collective-permute-start.6) | collective-permute-done | bytes 90144 | tf_op jit(solution)/shard_map/ppermute | solution.py:634
  21.8 0.5 %shard_map.83 = (f32[72,768]{1,0:T(8,128)S(1)}, f32[22,8,128]{2,1,0:T(8,128)S(1)}) custom-call(f32[6,72,768]{2,1,0:T(8,128)S(1)} %shard_map.81.after.inner.refs_2_, f32[22,8,128]{2,1,0:T(8,128)S(1)} %collective-permute-done.6.refs_0_, f32[72,768]{1,0:T(8,128)S(1)} %get-tuple-element.62.edge_b.refs_1_, f32[6,72,768]{2,1,0:T(8,128)S(1)} %shard_map.79.after.inner.refs_2_, ...), custom_call_target="tpu_custom_call" | custom-call | flops 67108864 | tf_op jit(solution)/shard_map/pallas_call | solution.py:587
  22.3 1.5 %collective-permute-start.9 = (f32[22,8,128]{2,1,0:T(8,128)S(1)}, f32[22,8,128]{2,1,0:T(8,128)S(1)}, u32[]{:S(2)}, u32[]{:S(2)}) collective-permute-start(f32[22,8,128]{2,1,0:T(8,128)S(1)} %get-tuple-element.70), channel_id=1, source_target_pairs={{8,16},{16,8},{24,0},{0,24},{9,17},{17,9},{25,1},{1,25},{10,18},{1... | collective-permute-start | bytes 270344 | tf_op jit(solution)/shard_map/ppermute | solution.py:634
  23.8 0.0 collective-permute-done.5.refs_0_
  23.8 0.5 %shard_map.82 = (f32[72,768]{1,0:T(8,128)S(1)}, f32[22,8,128]{2,1,0:T(8,128)S(1)}) custom-call(f32[6,72,768]{2,1,0:T(8,128)S(1)} %shard_map.81.after.inner.refs_2_, f32[22,8,128]{2,1,0:T(8,128)S(1)} %collective-permute-done.5.refs_0_, f32[72,768]{1,0:T(8,128)S(1)} %get-tuple-element.58.edge_a.refs_1_, f32[6,72,768]{2,1,0:T(8,128)S(1)} %shard_map.79.after.inner.refs_2_, ...), custom_call_target="tpu_custom_call" | custom-call | flops 67108864 | tf_op jit(solution)/shard_map/pallas_call | solution.py:587
  24.2 1.9 %collective-permute-start.7 = (f32[22,8,128]{2,1,0:T(8,128)S(1)}, f32[22,8,128]{2,1,0:T(8,128)S(1)}, u32[]{:S(2)}, u32[]{:S(2)}) collective-permute-start(f32[22,8,128]{2,1,0:T(8,128)S(1)} %get-tuple-element.67), channel_id=1, source_target_pairs={{0,8},{8,0},{16,24},{24,16},{1,9},{9,1},{17,25},{25,17},{2,10},{10... | collective-permute-start | bytes 270344 | tf_op jit(solution)/shard_map/ppermute | solution.py:635
  26.2 1.0 %shard_map.84.after.inner.refs_2_ = f32[6,72,768]{2,1,0:T(8,128)S(1)} custom-call(f32[72,768]{1,0:T(8,128)S(1)} %get-tuple-element.64.edge_a.refs_1_, f32[72,768]{1,0:T(8,128)S(1)} %get-tuple-element.66.edge_b.refs_1_, f32[6,72,768]{2,1,0:T(8,128)S(1)} %shard_map.81.after.inner.refs_2_, f32[8,72,128]{2,1,0:T(8,128)S(1)} %get-tuple-element.53.seas.refs_3_, ...), custom_call_target="tpu_custom_call" | custom-call | flops 268435456 | tf_op jit(solution)/shard_map/pallas_call | solution.py:587
  27.2 1.2 %collective-permute-done.9.refs_0_ = f32[22,8,128]{2,1,0:T(8,128)S(1)} collective-permute-done((f32[22,8,128]{2,1,0:T(8,128)S(1)}, f32[22,8,128]{2,1,0:T(8,128)S(1)}, u32[]{:S(2)}, u32[]{:S(2)}) %collective-permute-start.9) | collective-permute-done | bytes 90144 | tf_op jit(solution)/shard_map/ppermute | solution.py:634
  28.4 0.5 %shard_map.86 = (f32[72,768]{1,0:T(8,128)S(1)}, f32[21,8,128]{2,1,0:T(8,128)S(1)}) custom-call(f32[6,72,768]{2,1,0:T(8,128)S(1)} %shard_map.84.after.inner.refs_2_, f32[22,8,128]{2,1,0:T(8,128)S(1)} %collective-permute-done.9.refs_0_, f32[72,768]{1,0:T(8,128)S(1)} %get-tuple-element.66.edge_b.refs_1_, f32[6,72,768]{2,1,0:T(8,128)S(1)} %shard_map.81.after.inner.refs_2_, ...), custom_call_target="tpu_custom_call" | custom-call | flops 67108864 | tf_op jit(solution)/shard_map/pallas_call | solution.py:587
  28.9 1.8 %collective-permute-start.10 = (f32[21,8,128]{2,1,0:T(8,128)S(1)}, f32[21,8,128]{2,1,0:T(8,128)S(1)}, u32[]{:S(2)}, u32[]{:S(2)}) collective-permute-start(f32[21,8,128]{2,1,0:T(8,128)S(1)} %get-tuple-element.72), channel_id=1, source_target_pairs={{8,16},{16,8},{24,0},{0,24},{9,17},{17,9},{25,1},{1,25},{10,18},{1... | collective-permute-start | bytes 258056 | tf_op jit(solution)/shard_map/ppermute | solution.py:634
  30.6 0.0 collective-permute-done.7.refs_0_
  30.6 0.5 %shard_map.85 = (f32[72,768]{1,0:T(8,128)S(1)}, f32[21,8,128]{2,1,0:T(8,128)S(1)}) custom-call(f32[6,72,768]{2,1,0:T(8,128)S(1)} %shard_map.84.after.inner.refs_2_, f32[22,8,128]{2,1,0:T(8,128)S(1)} %collective-permute-done.7.refs_0_, f32[72,768]{1,0:T(8,128)S(1)} %get-tuple-element.64.edge_a.refs_1_, f32[6,72,768]{2,1,0:T(8,128)S(1)} %shard_map.81.after.inner.refs_2_, ...), custom_call_target="tpu_custom_call" | custom-call | flops 67108864 | tf_op jit(solution)/shard_map/pallas_call | solution.py:587
  31.1 1.0 %collective-permute-start.8 = (f32[21,8,128]{2,1,0:T(8,128)S(1)}, f32[21,8,128]{2,1,0:T(8,128)S(1)}, u32[]{:S(2)}, u32[]{:S(2)}) collective-permute-start(f32[21,8,128]{2,1,0:T(8,128)S(1)} %get-tuple-element.68), channel_id=1, source_target_pairs={{0,8},{8,0},{16,24},{24,16},{1,9},{9,1},{17,25},{25,17},{2,10},{10... | collective-permute-start | bytes 258056 | tf_op jit(solution)/shard_map/ppermute | solution.py:635
  32.1 0.9 %shard_map.87.after.done_inner = f32[6,64,648]{2,1,0:T(8,128)S(1)} custom-call(f32[72,768]{1,0:T(8,128)S(1)} %get-tuple-element.69.edge_a.edge, f32[72,768]{1,0:T(8,128)S(1)} %get-tuple-element.71.edge_b.refs_1_, f32[6,72,768]{2,1,0:T(8,128)S(1)} %shard_map.84.after.inner.refs_2_, f32[8,72,128]{2,1,0:T(8,128)S(1)} %get-tuple-element.53.seas.refs_3_, ...), custom_call_target="tpu_custom_call" | custom-call | flops 268435456 | tf_op jit(solution)/shard_map/pallas_call | solution.py:587
  33.0 1.3 %collective-permute-done.10.refs_0_ = f32[21,8,128]{2,1,0:T(8,128)S(1)} collective-permute-done((f32[21,8,128]{2,1,0:T(8,128)S(1)}, f32[21,8,128]{2,1,0:T(8,128)S(1)}, u32[]{:S(2)}, u32[]{:S(2)}) %collective-permute-start.10) | collective-permute-done | bytes 86048 | tf_op jit(solution)/shard_map/ppermute | solution.py:634
  34.3 0.4 %shard_map.88.done_edge = f32[64,648]{1,0:T(8,128)S(1)} custom-call(f32[6,64,648]{2,1,0:T(8,128)S(1)} %shard_map.87.after.done_inner, f32[21,8,128]{2,1,0:T(8,128)S(1)} %collective-permute-done.10.refs_0_, f32[72,768]{1,0:T(8,128)S(1)} %get-tuple-element.71.edge_b.refs_1_, f32[6,72,768]{2,1,0:T(8,128)S(1)} %shard_map.84.after.inner.refs_2_, ...), custom_call_target="tpu_custom_call" | custom-call | flops 67108864 | tf_op jit(solution)/shard_map/pallas_call | solution.py:587
  34.7 0.9 %collective-permute-done.8.halo = f32[21,8,128]{2,1,0:T(8,128)S(1)} collective-permute-done((f32[21,8,128]{2,1,0:T(8,128)S(1)}, f32[21,8,128]{2,1,0:T(8,128)S(1)}, u32[]{:S(2)}, u32[]{:S(2)}) %collective-permute-start.8) | collective-permute-done | bytes 86048 | tf_op jit(solution)/shard_map/ppermute | solution.py:635
  35.6 1.2 %shard_map.89 = f32[8,64,648]{2,1,0:T(8,128)} custom-call(f32[21,8,128]{2,1,0:T(8,128)S(1)} %collective-permute-done.8.halo, f32[72,768]{1,0:T(8,128)S(1)} %get-tuple-element.69.edge_a.edge, f32[6,72,768]{2,1,0:T(8,128)S(1)} %shard_map.84.after.inner.refs_2_, f32[8,72,128]{2,1,0:T(8,128)S(1)} %get-tuple-element.53.seas.refs_3_, ...), custom_call_target="tpu_custom_call" | custom-call | flops 67108864 | tf_op jit(solution)/shard_map/pallas_call | solution.py:587
  (5 shorter events, 0.0 us)
Async XLA Ops:
  0.0 3.9 %copy-start.5 = (f32[8,64]{1,0:T(8,128)S(1)}, f32[8,64]{1,0:T(8,128)}, u32[]{:S(2)}) copy-start(f32[8,64]{1,0:T(8,128)} %wind_ref.1) | copy-start | bytes 6148
  0.0 3.9 %copy-start.4 = (s32[8,64]{1,0:T(8,128)S(1)}, s32[8,64]{1,0:T(8,128)}, u32[]{:S(2)}) copy-start(s32[8,64]{1,0:T(8,128)} %ice_ref.1) | copy-start | bytes 6148
  0.0 3.9 %copy-start.3 = (s32[8,64]{1,0:T(8,128)S(1)}, s32[8,64]{1,0:T(8,128)}, u32[]{:S(2)}) copy-start(s32[8,64]{1,0:T(8,128)} %sea_ref.1) | copy-start | bytes 6148
  0.0 3.9 %copy-start = (f32[8,64,648]{2,1,0:T(8,128)S(1)}, f32[8,64,648]{2,1,0:T(8,128)}, u32[]{:S(2)}) copy-start(f32[8,64,648]{2,1,0:T(8,128)} %spectrum.3) | copy-start | bytes 3981316
  0.0 4.6 %copy-start.2 = (f32[8,768]{1,0:T(8,128)S(1)}, f32[8,768]{1,0:T(8,128)}, u32[]{:S(2)}) copy-start(f32[8,768]{1,0:T(8,128)} %constant.2.clone.angle_ref) | copy-start | bytes 73732
  0.0 4.6 %copy-start.1 = (bf16[648,648]{1,0:T(8,128)(2,1)S(1)}, bf16[648,648]{1,0:T(8,128)(2,1)}, u32[]{:S(2)}) copy-start(bf16[648,648]{1,0:T(8,128)(2,1)} %coupling_ref.1) | copy-start | bytes 2519428
  0.0 4.6 %copy-start.6 = (f32[18]{0:T(128)S(1)}, f32[18]{0:T(128)}, u32[]{:S(2)}) copy-start(f32[18]{0:T(128)} %speed_ref.1) | copy-start | bytes 220
  1.4 4.1 %collective-permute-start = (f32[21,8,128]{2,1,0:T(8,128)S(1)}, f32[21,8,128]{2,1,0:T(8,128)S(1)}, u32[]{:S(2)}, u32[]{:S(2)}) collective-permute-start(f32[21,8,128]{2,1,0:T(8,128)S(1)} %get-tuple-element.39), channel_id=1, source_target_pairs={{0,1},{1,0},{2,3},{3,2},{4,5},{5,4},{6,7},{7,6},{8,9},{9,8},{10,11... | collective-permute-start | bytes 258056 | tf_op jit(solution)/shard_map/ppermute | solution.py:607
  1.4 5.8 %collective-permute-start.1 = (f32[21,8,128]{2,1,0:T(8,128)S(1)}, f32[21,8,128]{2,1,0:T(8,128)S(1)}, u32[]{:S(2)}, u32[]{:S(2)}) collective-permute-start(f32[21,8,128]{2,1,0:T(8,128)S(1)} %get-tuple-element.40), channel_id=1, source_target_pairs={{1,2},{2,1},{3,4},{4,3},{5,6},{6,5},{9,10},{10,9},{11,12},{12,11},... | collective-permute-start | bytes 258056 | tf_op jit(solution)/shard_map/ppermute | solution.py:606
  7.7 9.7 %collective-permute-start.2 = (f32[23,8,128]{2,1,0:T(8,128)S(1)}, f32[23,8,128]{2,1,0:T(8,128)S(1)}, u32[]{:S(2)}, u32[]{:S(2)}) collective-permute-start(f32[23,8,128]{2,1,0:T(8,128)S(1)} %get-tuple-element.50), channel_id=1, source_target_pairs={{0,8},{8,0},{16,24},{24,16},{1,9},{9,1},{17,25},{25,17},{2,10},{10... | collective-permute-start | bytes 282632 | tf_op jit(solution)/shard_map/ppermute | solution.py:635
  9.2 5.4 %collective-permute-start.4 = (f32[21,8,128]{2,1,0:T(8,128)S(1)}, f32[21,8,128]{2,1,0:T(8,128)S(1)}, u32[]{:S(2)}, u32[]{:S(2)}) collective-permute-start(f32[21,8,128]{2,1,0:T(8,128)S(1)} %get-tuple-element.61), channel_id=1, source_target_pairs={{8,16},{16,8},{24,0},{0,24},{9,17},{17,9},{25,1},{1,25},{10,18},{1... | collective-permute-start | bytes 258056 | tf_op jit(solution)/shard_map/ppermute | solution.py:634
  10.7 4.7 %collective-permute-start.3 = (f32[3,8,128]{2,1,0:T(8,128)S(1)}, f32[3,8,128]{2,1,0:T(8,128)S(1)}, u32[]{:S(2)}, u32[]{:S(2)}) collective-permute-start(f32[3,8,128]{2,1,0:T(8,128)S(1)} %get-tuple-element.60), channel_id=1, source_target_pairs={{8,16},{16,8},{24,0},{0,24},{9,17},{17,9},{25,1},{1,25},{10,18},{1... | collective-permute-start | bytes 36872 | tf_op jit(solution)/shard_map/ppermute | solution.py:637
  15.9 5.9 %collective-permute-start.6 = (f32[22,8,128]{2,1,0:T(8,128)S(1)}, f32[22,8,128]{2,1,0:T(8,128)S(1)}, u32[]{:S(2)}, u32[]{:S(2)}) collective-permute-start(f32[22,8,128]{2,1,0:T(8,128)S(1)} %get-tuple-element.65), channel_id=1, source_target_pairs={{8,16},{16,8},{24,0},{0,24},{9,17},{17,9},{25,1},{1,25},{10,18},{1... | collective-permute-start | bytes 270344 | tf_op jit(solution)/shard_map/ppermute | solution.py:634
  17.8 5.9 %collective-permute-start.5 = (f32[22,8,128]{2,1,0:T(8,128)S(1)}, f32[22,8,128]{2,1,0:T(8,128)S(1)}, u32[]{:S(2)}, u32[]{:S(2)}) collective-permute-start(f32[22,8,128]{2,1,0:T(8,128)S(1)} %get-tuple-element.63), channel_id=1, source_target_pairs={{0,8},{8,0},{16,24},{24,16},{1,9},{9,1},{17,25},{25,17},{2,10},{10... | collective-permute-start | bytes 270344 | tf_op jit(solution)/shard_map/ppermute | solution.py:635
  22.3 6.1 %collective-permute-start.9 = (f32[22,8,128]{2,1,0:T(8,128)S(1)}, f32[22,8,128]{2,1,0:T(8,128)S(1)}, u32[]{:S(2)}, u32[]{:S(2)}) collective-permute-start(f32[22,8,128]{2,1,0:T(8,128)S(1)} %get-tuple-element.70), channel_id=1, source_target_pairs={{8,16},{16,8},{24,0},{0,24},{9,17},{17,9},{25,1},{1,25},{10,18},{1... | collective-permute-start | bytes 270344 | tf_op jit(solution)/shard_map/ppermute | solution.py:634
  24.2 6.4 %collective-permute-start.7 = (f32[22,8,128]{2,1,0:T(8,128)S(1)}, f32[22,8,128]{2,1,0:T(8,128)S(1)}, u32[]{:S(2)}, u32[]{:S(2)}) collective-permute-start(f32[22,8,128]{2,1,0:T(8,128)S(1)} %get-tuple-element.67), channel_id=1, source_target_pairs={{0,8},{8,0},{16,24},{24,16},{1,9},{9,1},{17,25},{25,17},{2,10},{10... | collective-permute-start | bytes 270344 | tf_op jit(solution)/shard_map/ppermute | solution.py:635
  28.9 5.5 %collective-permute-start.10 = (f32[21,8,128]{2,1,0:T(8,128)S(1)}, f32[21,8,128]{2,1,0:T(8,128)S(1)}, u32[]{:S(2)}, u32[]{:S(2)}) collective-permute-start(f32[21,8,128]{2,1,0:T(8,128)S(1)} %get-tuple-element.72), channel_id=1, source_target_pairs={{8,16},{16,8},{24,0},{0,24},{9,17},{17,9},{25,1},{1,25},{10,18},{1... | collective-permute-start | bytes 258056 | tf_op jit(solution)/shard_map/ppermute | solution.py:634
  31.1 4.6 %collective-permute-start.8 = (f32[21,8,128]{2,1,0:T(8,128)S(1)}, f32[21,8,128]{2,1,0:T(8,128)S(1)}, u32[]{:S(2)}, u32[]{:S(2)}) collective-permute-start(f32[21,8,128]{2,1,0:T(8,128)S(1)} %get-tuple-element.68), channel_id=1, source_target_pairs={{0,8},{8,0},{16,24},{24,16},{1,9},{9,1},{17,25},{25,17},{2,10},{10... | collective-permute-start | bytes 258056 | tf_op jit(solution)/shard_map/ppermute | solution.py:635
